TPU v7x, 32 devices: a whole 2x2x4 slice. The times are simulated.
32 devices in a mesh: seq: 8 (over z, x), head: 4 (over y, core).
Axes of the slice: x: 2, y: 2, z: 4, core: 2. Of those that a mesh axis runs over, the one named last changes fastest.
Arguments:
- queries: bfloat16 [4096, 6144], P('seq', 'head'), may hold values from -10 to 10
- keys: bfloat16 [4096, 6144], P('seq', 'head'), may hold values from -10 to 10
- values: bfloat16 [4096, 6144], P('seq', 'head'), may hold values from -6 to 6
- frame_of_block: int32 [16], P('seq'), may hold values from 0 to 7, never falling along the last dimension, each value on 1 to 4 neighbouring positions
- pair_mask: int32 [16, 16], P('seq'), may hold values 0 or 1
- w_out: bfloat16 [6144, 6144], P('head', 'seq'), may hold values from -0.4375 to 0.4375
Outputs:
- projected: bfloat16 [4096, 6144], P('seq', 'head')
Inputs may be any that keep to these rules, and one draw needn't show every extreme that they name: `frame_of_block`: frame ids never fall along the blocks, every frame spans 1 to 4 consecutive blocks.
All inputs are finite; a program needn't handle non-finite values. No bound on the sum of `pair_mask` on one device may be relied on, other than what follows from the above.
Results may differ from a plain program's by a relative error of at most 0.015.
Values may be sent and summed in bfloat16 or wider, within the bound.
A program may use at most 192 MiB of HBM per device.

v0:
```python
import math

import jax
import jax.numpy as jnp
from jax import lax
from jax.sharding import PartitionSpec as P

HD = 128
BLK = 256


def body(queries, keys, values, frame_of_block, pair_mask, w_out):
    tok = queries.shape[0]
    heads_here = queries.shape[1] // HD
    count_blocks = pair_mask.shape[1]
    scale = 1.0 / math.sqrt(HD)
    key_span = 512
    q_heads = queries.reshape(tok, heads_here, HD)
    q_frame = jnp.repeat(frame_of_block, BLK)
    mask_rows = jnp.repeat(pair_mask.astype(jnp.float32), BLK, axis=0)
    block_ids = jnp.arange(count_blocks, dtype=jnp.int32)

    def update(state, k_rows, v_rows, allowed):
        peak, total, accum = state
        k_heads = k_rows.reshape(k_rows.shape[0], heads_here, HD)
        v_heads = v_rows.reshape(v_rows.shape[0], heads_here, HD)
        score = (
            jnp.einsum("qhd,khd->hqk", q_heads, k_heads, preferred_element_type=jnp.float32) * scale
        )
        score = jnp.where(allowed[None], score, -1e30)
        new_peak = jnp.maximum(peak, jnp.max(score, axis=2))
        weight = jnp.where(allowed[None], jnp.exp(score - new_peak[:, :, None]), 0.0)
        factor = jnp.exp(peak - new_peak)
        new_total = total * factor + jnp.sum(weight, axis=2)
        added = jnp.einsum(
            "hqk,khd->qhd", weight.astype(jnp.bfloat16), v_heads, preferred_element_type=jnp.float32
        )
        new_accum = accum * factor.T[:, :, None] + added
        return (new_peak, new_total, new_accum)

    def attend_block(state, k_rows, v_rows, k_frame, start):
        count = k_rows.shape[0]
        k_block = (start + jnp.arange(count, dtype=jnp.int32)) // BLK
        one_hot = (block_ids[:, None] == k_block[None, :]).astype(jnp.float32)
        link = jnp.dot(mask_rows, one_hot, preferred_element_type=jnp.float32)
        same = k_frame[None, :] == q_frame[:, None]
        allowed = (k_frame[None, :] <= q_frame[:, None]) & ((link > 0.5) | same)
        return update(state, k_rows, v_rows, allowed)

    initial = (
        jnp.full((heads_here, tok), -1e30, jnp.float32),
        jnp.zeros((heads_here, tok), jnp.float32),
        jnp.zeros((tok, heads_here, HD), jnp.float32),
    )
    k_frame_local = jnp.repeat(frame_of_block, BLK)
    k_rows = lax.all_gather(keys, "seq", axis=0, tiled=True)
    v_rows = lax.all_gather(values, "seq", axis=0, tiled=True)
    k_frame = lax.all_gather(k_frame_local, "seq", axis=0, tiled=True)
    count = k_rows.shape[0]

    def step(index, inner):
        offset = (index * key_span).astype(jnp.int32)
        return attend_block(
            inner,
            lax.dynamic_slice_in_dim(k_rows, offset, key_span, 0),
            lax.dynamic_slice_in_dim(v_rows, offset, key_span, 0),
            lax.dynamic_slice_in_dim(k_frame, offset, key_span, 0),
            offset,
        )

    state = lax.fori_loop(0, count // key_span, step, initial)
    peak, total, accum = state
    attn = (accum / total.T[:, :, None]).reshape(tok, heads_here * HD).astype(jnp.bfloat16)
    terms = jnp.dot(
        attn, lax.all_gather(w_out, "seq", axis=1, tiled=True), preferred_element_type=jnp.float32
    )
    return lax.psum_scatter(terms.astype(jnp.bfloat16), "head", scatter_dimension=1, tiled=True)


def solution(mesh):
    placed = (
        P("seq", "head"),
        P("seq", "head"),
        P("seq", "head"),
        P("seq"),
        P("seq", None),
        P("head", "seq"),
    )
    return jax.shard_map(
        body, mesh=mesh, in_specs=placed, out_specs=P("seq", "head"), check_vma=False
    )
```

profile of v0, /device:TPU:1, one launch (start us, length us, event | category | flops | bytes accessed | tf_op | source)
XLA Modules:
  0.0 806.4 jit_solution(6344681956070175364)
XLA Ops:
  14.5 24.2 %all-gather = s32[8,1,512]{2,1,0:T(1,128)S(1)} all-gather(s32[1,1,512]{2,1,0:T(1,128)S(1)} %reshape.60), channel_id=1, replica_groups=mesh['seq'=8,'head'=4] {'seq'}, dimensions={0}, use_global_device_ids=true | all-gather | bytes 18432 | tf_op jit(solution)/shard_map/all_gather | solution.py:58
  38.7 148.3 %all-gather.5.cloned.1.call-done = bf16[4096,1536]{0,1:T(8,128)(2,1)} async-done(((bf16[512,1536]{0,1:T(8,128)(2,1)}), bf16[4096,1536]{0,1:T(8,128)(2,1)}) %all-gather.5.cloned.1.call-update) | async-done | bytes 12582928 | tf_op jit(solution)/shard_map/all_gather | solution.py:56
  187.0 176.4 %all-gather.7.cloned.1.call-done = bf16[4096,1536]{0,1:T(8,128)(2,1)} async-done(((bf16[512,1536]{0,1:T(8,128)(2,1)}), bf16[4096,1536]{0,1:T(8,128)(2,1)}) %all-gather.7.cloned.1.call-update) | async-done | bytes 12582928 | tf_op jit(solution)/shard_map/all_gather | solution.py:57
  363.4 191.9 %while.20 = (s32[]{:T(128)}, f32[12,512]{1,0:T(8,128)S(1)}, f32[12,512]{1,0:T(8,128)S(1)}, f32[512,12,128]{0,2,1:T(8,128)}, s32[4096]{0:T(1024)S(1)}, /*index=5*...) while((s32[]{:T(128)}, f32[12,512]{1,0:T(8,128)S(1)}, ...), condition=%wide.region_3.4_spmd.clone, body=%wide.region_0.3_spmd.clone.sunk | while | flops 1663627264 | bytes 106875176 | solution.py:71
  366.1 7.3 fusion.52
  373.5 10.2 %bitcast_add_fusion.2 = f32[512,12,128]{0,2,1:T(8,128)} fusion(f32[512,12,128]{0,2,1:T(8,128)} %get-tuple-element.450, bf16[512,12,128]{0,2,1:T(8,128)(2,1)S(1)} %bitcast.70, f32[12,512,512]{2,1,0:T(8,128)} %get-tuple-element.430, f32[12,512]{1,0:T(8,128)S(1)} %get-tuple-element.462, pred[512,512]{0,1:T(8,128)(4,1)S(1)} %fusion.51, ...), kind=kOutput, calls=%fused_computation.10.clone.1 | convolution fusion | flops 823394304 | bytes 20758528 | tf_op jit(solution)/shard_map/while/body/eval_jaxpr/hqk,khd->qhd/dot_general | solution.py:35
  389.7 6.9 fusion.52
  396.6 11.1 %bitcast_add_fusion.2 = f32[512,12,128]{0,2,1:T(8,128)} fusion(f32[512,12,128]{0,2,1:T(8,128)} %get-tuple-element.450, bf16[512,12,128]{0,2,1:T(8,128)(2,1)S(1)} %bitcast.70, f32[12,512,512]{2,1,0:T(8,128)} %get-tuple-element.430, f32[12,512]{1,0:T(8,128)S(1)} %get-tuple-element.462, pred[512,512]{0,1:T(8,128)(4,1)S(1)} %fusion.51, ...), kind=kOutput, calls=%fused_computation.10.clone.1 | convolution fusion | flops 823394304 | bytes 20758528 | tf_op jit(solution)/shard_map/while/body/eval_jaxpr/hqk,khd->qhd/dot_general | solution.py:35
  413.6 6.9 fusion.52
  420.5 11.1 %bitcast_add_fusion.2 = f32[512,12,128]{0,2,1:T(8,128)} fusion(f32[512,12,128]{0,2,1:T(8,128)} %get-tuple-element.450, bf16[512,12,128]{0,2,1:T(8,128)(2,1)S(1)} %bitcast.70, f32[12,512,512]{2,1,0:T(8,128)} %get-tuple-element.430, f32[12,512]{1,0:T(8,128)S(1)} %get-tuple-element.462, pred[512,512]{0,1:T(8,128)(4,1)S(1)} %fusion.51, ...), kind=kOutput, calls=%fused_computation.10.clone.1 | convolution fusion | flops 823394304 | bytes 20758528 | tf_op jit(solution)/shard_map/while/body/eval_jaxpr/hqk,khd->qhd/dot_general | solution.py:35
  431.6 3.1 fusion.54
  437.6 6.9 fusion.52
  444.5 11.1 %bitcast_add_fusion.2 = f32[512,12,128]{0,2,1:T(8,128)} fusion(f32[512,12,128]{0,2,1:T(8,128)} %get-tuple-element.450, bf16[512,12,128]{0,2,1:T(8,128)(2,1)S(1)} %bitcast.70, f32[12,512,512]{2,1,0:T(8,128)} %get-tuple-element.430, f32[12,512]{1,0:T(8,128)S(1)} %get-tuple-element.462, pred[512,512]{0,1:T(8,128)(4,1)S(1)} %fusion.51, ...), kind=kOutput, calls=%fused_computation.10.clone.1 | convolution fusion | flops 823394304 | bytes 20758528 | tf_op jit(solution)/shard_map/while/body/eval_jaxpr/hqk,khd->qhd/dot_general | solution.py:35
  461.5 6.9 fusion.52
  468.4 11.2 %bitcast_add_fusion.2 = f32[512,12,128]{0,2,1:T(8,128)} fusion(f32[512,12,128]{0,2,1:T(8,128)} %get-tuple-element.450, bf16[512,12,128]{0,2,1:T(8,128)(2,1)S(1)} %bitcast.70, f32[12,512,512]{2,1,0:T(8,128)} %get-tuple-element.430, f32[12,512]{1,0:T(8,128)S(1)} %get-tuple-element.462, pred[512,512]{0,1:T(8,128)(4,1)S(1)} %fusion.51, ...), kind=kOutput, calls=%fused_computation.10.clone.1 | convolution fusion | flops 823394304 | bytes 20758528 | tf_op jit(solution)/shard_map/while/body/eval_jaxpr/hqk,khd->qhd/dot_general | solution.py:35
  485.5 6.9 fusion.52
  492.4 11.3 %bitcast_add_fusion.2 = f32[512,12,128]{0,2,1:T(8,128)} fusion(f32[512,12,128]{0,2,1:T(8,128)} %get-tuple-element.450, bf16[512,12,128]{0,2,1:T(8,128)(2,1)S(1)} %bitcast.70, f32[12,512,512]{2,1,0:T(8,128)} %get-tuple-element.430, f32[12,512]{1,0:T(8,128)S(1)} %get-tuple-element.462, pred[512,512]{0,1:T(8,128)(4,1)S(1)} %fusion.51, ...), kind=kOutput, calls=%fused_computation.10.clone.1 | convolution fusion | flops 823394304 | bytes 20758528 | tf_op jit(solution)/shard_map/while/body/eval_jaxpr/hqk,khd->qhd/dot_general | solution.py:35
  509.7 6.9 fusion.52
  516.6 11.3 %bitcast_add_fusion.2 = f32[512,12,128]{0,2,1:T(8,128)} fusion(f32[512,12,128]{0,2,1:T(8,128)} %get-tuple-element.450, bf16[512,12,128]{0,2,1:T(8,128)(2,1)S(1)} %bitcast.70, f32[12,512,512]{2,1,0:T(8,128)} %get-tuple-element.430, f32[12,512]{1,0:T(8,128)S(1)} %get-tuple-element.462, pred[512,512]{0,1:T(8,128)(4,1)S(1)} %fusion.51, ...), kind=kOutput, calls=%fused_computation.10.clone.1 | convolution fusion | flops 823394304 | bytes 20758528 | tf_op jit(solution)/shard_map/while/body/eval_jaxpr/hqk,khd->qhd/dot_general | solution.py:35
  533.9 6.9 fusion.52
  540.8 11.3 %bitcast_add_fusion.2 = f32[512,12,128]{0,2,1:T(8,128)} fusion(f32[512,12,128]{0,2,1:T(8,128)} %get-tuple-element.450, bf16[512,12,128]{0,2,1:T(8,128)(2,1)S(1)} %bitcast.70, f32[12,512,512]{2,1,0:T(8,128)} %get-tuple-element.430, f32[12,512]{1,0:T(8,128)S(1)} %get-tuple-element.462, pred[512,512]{0,1:T(8,128)(4,1)S(1)} %fusion.51, ...), kind=kOutput, calls=%fused_computation.10.clone.1 | convolution fusion | flops 823394304 | bytes 20758528 | tf_op jit(solution)/shard_map/while/body/eval_jaxpr/hqk,khd->qhd/dot_general | solution.py:35
  557.7 168.5 %all-gather.9.cloned.1.call-done = bf16[1536,6144]{1,0:T(8,128)(2,1)} async-done(((bf16[1536,768]{1,0:T(8,128)(2,1)}), bf16[1536,6144]{1,0:T(8,128)(2,1)}) %all-gather.9.cloned.1.call-update) | async-done | bytes 18874384 | tf_op jit(solution)/shard_map/all_gather | solution.py:75
  726.2 15.7 %convolution_convert_fusion = bf16[512,6144]{1,0:T(8,128)(2,1)} fusion(bf16[512,1536]{0,1:T(8,128)(2,1)S(1)} %bitcast.73, bf16[1536,6144]{1,0:T(8,128)(2,1)} %all-gather.9.cloned.1.call-done), kind=kOutput, calls=%fused_computation.39 | convolution fusion | flops 9666822144 | bytes 26738688 | tf_op jit(solution)/shard_map/dot_general | solution.py:74
  741.9 58.0 %reduce-scatter.2.cloned.1.call-done = bf16[512,1536]{1,0:T(8,128)(2,1)} async-done(((bf16[512,6144]{1,0:T(8,128)(2,1)}), bf16[512,1536]{1,0:T(8,128)(2,1)}) %reduce-scatter.2.cloned.1.call-update) | async-done | bytes 1572880 | tf_op jit(solution)/shard_map/reduce_scatter | solution.py:77
  (128 shorter events, 54.3 us)
Async XLA Ops:
  6.5 2.8 copy-start.1
  6.5 180.5 %all-gather.5.cloned.1.call-start = ((), (), s32[]{:S(2)}) async-start(), calls=%async_computation.1 | async-start | bytes 14155776 | tf_op jit(solution)/shard_map/all_gather | solution.py:56
  9.3 354.1 %all-gather.7.cloned.1.call-start = ((), (), s32[]{:S(2)}) async-start(), calls=%async_computation.2 | async-start | bytes 14155776 | tf_op jit(solution)/shard_map/all_gather | solution.py:57
  10.9 715.2 %all-gather.9.cloned.1.call-start = ((), (), s32[]{:S(2)}) async-start(), calls=%async_computation.3 | async-start | bytes 21233664 | tf_op jit(solution)/shard_map/all_gather | solution.py:75
  11.7 788.2 %reduce-scatter.2.cloned.1.call-start = ((), (), s32[]{:S(2)}) async-start(), calls=%async_computation.4 | async-start | bytes 7864320 | tf_op jit(solution)/shard_map/reduce_scatter | solution.py:77
  11.7 2.7 copy-start.2
  11.8 26.9 %copy-start.3 = (s32[2,16]{1,0:T(2,128)S(1)}, s32[2,16]{1,0:T(2,128)}, u32[]{:S(2)}) copy-start(s32[2,16]{1,0:T(2,128)} %param.12) | copy-start | bytes 388
  373.5 10.2 %copy-start = (f32[12,512,512]{2,1,0:T(8,128)S(1)}, f32[12,512,512]{2,1,0:T(8,128)}, u32[]{:S(2)}) copy-start(f32[12,512,512]{2,1,0:T(8,128)} %get-tuple-element.430) | copy-start | bytes 37748740 | tf_op jit(solution)/shard_map/while
  396.5 11.1 %copy-start = (f32[12,512,512]{2,1,0:T(8,128)S(1)}, f32[12,512,512]{2,1,0:T(8,128)}, u32[]{:S(2)}) copy-start(f32[12,512,512]{2,1,0:T(8,128)} %get-tuple-element.430) | copy-start | bytes 37748740 | tf_op jit(solution)/shard_map/while
  420.5 11.1 %copy-start = (f32[12,512,512]{2,1,0:T(8,128)S(1)}, f32[12,512,512]{2,1,0:T(8,128)}, u32[]{:S(2)}) copy-start(f32[12,512,512]{2,1,0:T(8,128)} %get-tuple-element.430) | copy-start | bytes 37748740 | tf_op jit(solution)/shard_map/while
  444.4 11.1 %copy-start = (f32[12,512,512]{2,1,0:T(8,128)S(1)}, f32[12,512,512]{2,1,0:T(8,128)}, u32[]{:S(2)}) copy-start(f32[12,512,512]{2,1,0:T(8,128)} %get-tuple-element.430) | copy-start | bytes 37748740 | tf_op jit(solution)/shard_map/while
  468.4 11.2 %copy-start = (f32[12,512,512]{2,1,0:T(8,128)S(1)}, f32[12,512,512]{2,1,0:T(8,128)}, u32[]{:S(2)}) copy-start(f32[12,512,512]{2,1,0:T(8,128)} %get-tuple-element.430) | copy-start | bytes 37748740 | tf_op jit(solution)/shard_map/while
  492.4 11.3 %copy-start = (f32[12,512,512]{2,1,0:T(8,128)S(1)}, f32[12,512,512]{2,1,0:T(8,128)}, u32[]{:S(2)}) copy-start(f32[12,512,512]{2,1,0:T(8,128)} %get-tuple-element.430) | copy-start | bytes 37748740 | tf_op jit(solution)/shard_map/while
  516.6 11.3 %copy-start = (f32[12,512,512]{2,1,0:T(8,128)S(1)}, f32[12,512,512]{2,1,0:T(8,128)}, u32[]{:S(2)}) copy-start(f32[12,512,512]{2,1,0:T(8,128)} %get-tuple-element.430) | copy-start | bytes 37748740 | tf_op jit(solution)/shard_map/while
  540.8 11.3 %copy-start = (f32[12,512,512]{2,1,0:T(8,128)S(1)}, f32[12,512,512]{2,1,0:T(8,128)}, u32[]{:S(2)}) copy-start(f32[12,512,512]{2,1,0:T(8,128)} %get-tuple-element.430) | copy-start | bytes 37748740 | tf_op jit(solution)/shard_map/while
Sparse Core Ops, SparseCore 0:
  9.4 177.6 all-gather.4
  189.1 174.2 all-gather.6
  365.0 361.1 all-gather.8
  742.0 57.8 reduce-scatter.1
where the time goes:
time: 807 us; the launch traced here: 806 us
  waiting for transfers between devices  552 us (68%)
  matrix products  163 us (20%)
  other arithmetic  27.8 us (3%)
  local copies, waits for them, and re-layouts  25.3 us (3%)
  blocking collectives  24.2 us (3%)
  between operations  13.2 us (2%)
    all_gather x1, waiting for transfers between devices, body(): v_rows = lax.all_gather(values, 'seq', axis=0, tiled=True)  176 us
    all_gather x1, waiting for transfers between devices, body(): lax.all_gather(w_out, 'seq', axis=1, tiled=True)  169 us
    all_gather x1, waiting for transfers between devices, body(): k_rows = lax.all_gather(keys, 'seq', axis=0, tiled=True)  148 us
    dot_general x8, matrix products, update(): jnp.einsum('hqk,khd->qhd', weight.astype(jnp.bfloat16), v_heads, preferre...  88.7 us
    reduce_scatter x1, waiting for transfers between devices, body(): lax.psum_scatter(terms.astype(jnp.bfloat16), 'head', scatter_dimension=1,...  58 us
    dot_general x8, matrix products, update(): jnp.einsum('qhd,khd->hqk', q_heads, k_heads, preferred_element_type=jnp.f...  55.4 us
    reduce_sum x8, other arithmetic, update(): new_total = total * factor + jnp.sum(weight, axis=2)  25.1 us
    all_gather x1, blocking collectives, body(): k_frame = lax.all_gather(k_frame_local, 'seq', axis=0, tiled=True)  24.2 us
  transfers between devices with their start and end apart: 4, of which 4 were waited for; matrix products, arithmetic and copies ran while one was open for 25% of the time, Pallas kernels for 0%

commit v1 on v0

--- a/solution.py
+++ b/solution.py
@@ -1,15 +1,19 @@
+import functools
 import math
 
 import jax
 import jax.numpy as jnp
 from jax import lax
+from jax.experimental import pallas as pl
+from jax.experimental.pallas import tpu as pltpu
 from jax.sharding import PartitionSpec as P
 
 HD = 128
 BLK = 256
-
-
-def body(queries, keys, values, frame_of_block, pair_mask, w_out):
+NEG = -1e30
+
+
+def body_gather(queries, keys, values, frame_of_block, pair_mask, w_out):
     tok = queries.shape[0]
     heads_here = queries.shape[1] // HD
     count_blocks = pair_mask.shape[1]
@@ -77,6 +81,243 @@
     return lax.psum_scatter(terms.astype(jnp.bfloat16), "head", scatter_dimension=1, tiled=True)
 
 
+def greet(n, me):
+    barrier = pltpu.get_barrier_semaphore()
+    for k in range(1, n):
+        pl.semaphore_signal(barrier, inc=1, device_id={"seq": lax.rem(me + k, n)}, device_id_type=pl.DeviceIdType.MESH)
+    pl.semaphore_wait(barrier, n - 1)
+
+
+def cols(head):
+    return pl.ds(pl.multiple_of(head * HD, HD), HD)
+
+
+def rows(start, size):
+    return pl.ds(pl.multiple_of(start, size), size)
+
+
+def spread_kernel(n, tok, q, k, v, meta, qf, qs, kf, ks, vf, vs, metas, hold, hold_half, hold_meta, send, recv, here):
+    me = lax.axis_index("seq")
+    half = tok // 2
+
+    def pieces(to):
+        pair, odd = to // 2, lax.rem(to, 2)
+        own, shared = cols(3 * pair + 2 * odd), cols(3 * pair + 1)
+        full = rows(me * tok, tok)
+        return [
+            (meta, metas.at[rows(me * 8, 8)]),
+            (q.at[:, own], qf.at[full]),
+            (k.at[:, own], kf.at[full]),
+            (v.at[:, own], vf.at[full]),
+            (q.at[rows(odd * half, half), shared], qs.at[rows(me * half, half)]),
+            (k.at[:, shared], ks.at[full]),
+            (v.at[:, shared], vs.at[full]),
+        ]
+
+    def bounce(index):
+        if index == 0:
+            return hold_meta
+        if index == 4:
+            return hold_half
+        return hold.at[{1: 0, 2: 1, 3: 2, 5: 3, 6: 4}[index]]
+
+    greet(n, me)
+    copies = []
+    for step in range(1, n):
+        to = lax.rem(me + step, n)
+        for i, (src, dst) in enumerate(pieces(to)):
+            copy = pltpu.make_async_remote_copy(
+                src_ref=src, dst_ref=dst, send_sem=send.at[step - 1, i], recv_sem=recv.at[step - 1, i],
+                device_id={"seq": to}, device_id_type=pl.DeviceIdType.MESH,
+            )
+            copy.start()
+            copies.append(copy)
+    mine = pieces(me)
+    ins = [pltpu.make_async_copy(src, bounce(i), here.at[0, i]) for i, (src, _) in enumerate(mine)]
+    outs = [pltpu.make_async_copy(bounce(i), dst, here.at[1, i]) for i, (_, dst) in enumerate(mine)]
+    for c in ins:
+        c.start()
+    for c, d in zip(ins, outs):
+        c.wait()
+        d.start()
+    for d in outs:
+        d.wait()
+    for c in copies:
+        c.wait()
+
+
+def return_kernel(n, tok, of, os, attn, hold, hold_half, send, recv, here):
+    me = lax.axis_index("seq")
+    half = tok // 2
+    pair, odd = me // 2, lax.rem(me, 2)
+    own, shared = cols(3 * pair + 2 * odd), cols(3 * pair + 1)
+
+    def pieces(to):
+        return [
+            (of.at[rows(to * tok, tok)], attn.at[:, own]),
+            (os.at[rows(to * half, half)], attn.at[rows(odd * half, half), shared]),
+        ]
+
+    greet(n, me)
+    copies = []
+    for step in range(1, n):
+        to = lax.rem(me + step, n)
+        for i, (src, dst) in enumerate(pieces(to)):
+            copy = pltpu.make_async_remote_copy(
+                src_ref=src, dst_ref=dst, send_sem=send.at[step - 1, i], recv_sem=recv.at[step - 1, i],
+                device_id={"seq": to}, device_id_type=pl.DeviceIdType.MESH,
+            )
+            copy.start()
+            copies.append(copy)
+    for i, ((src, dst), via) in enumerate(zip(pieces(me), (hold, hold_half))):
+        c = pltpu.make_async_copy(src, via, here.at[0, i])
+        c.start()
+        c.wait()
+        d = pltpu.make_async_copy(via, dst, here.at[1, i])
+        d.start()
+        d.wait()
+    for c in copies:
+        c.wait()
+
+
+def attend_kernel(odd_ref, count_ref, list_ref, qf, qs, kf, ks, vf, vs, of, os):
+    odd = odd_ref[0]
+    j = pl.program_id(0)
+    factor = math.log2(math.e) / math.sqrt(HD)
+
+    def scores(q, k):
+        return lax.dot_general(q, k, (((1,), (1,)), ((), ())), preferred_element_type=jnp.float32)
+
+    def fold(state, parts, vals):
+        peak, total, accum = state
+        top = parts[0]
+        for s in parts[1:]:
+            top = jnp.maximum(top, s)
+        new_peak = jnp.maximum(peak, jnp.max(top, axis=1, keepdims=True))
+        keep = jnp.exp2((peak - new_peak) * factor)
+        total, accum = total * keep, accum * keep
+        for s, v in zip(parts, vals):
+            p = jnp.exp2((s - new_peak) * factor)
+            for c in range(0, BLK, HD):
+                total = total + p[:, c:c + HD]
+            accum = accum + jnp.dot(p.astype(jnp.bfloat16), v, preferred_element_type=jnp.float32)
+        return new_peak, total, accum
+
+    def start():
+        return (
+            jnp.full((BLK, 1), NEG, jnp.float32),
+            jnp.zeros((BLK, HD), jnp.float32),
+            jnp.zeros((BLK, HD), jnp.float32),
+        )
+
+    def finish(state):
+        _, total, accum = state
+        return (accum / jnp.sum(total, axis=1, keepdims=True)).astype(jnp.bfloat16)
+
+    def walk(block, streams):
+        count = count_ref[block]
+
+        def step(i, states):
+            a = rows(list_ref[block, 2 * i] * BLK, BLK)
+            b = rows(list_ref[block, 2 * i + 1] * BLK, BLK)
+            bias = jnp.where(2 * i + 1 < count, 0.0, NEG).astype(jnp.float32)
+            parts = [[scores(q, k[a, :]), scores(q, k[b, :]) + bias] for q, k, _ in streams]
+            return tuple(
+                fold(state, part, (v[a, :], v[b, :])) for state, part, (_, _, v) in zip(states, parts, streams)
+            )
+
+        return lax.fori_loop(0, (count + 1) // 2, step, tuple(start() for _ in streams))
+
+    same, other = rows(odd * BLK, BLK), rows((1 - odd) * BLK, BLK)
+    first, second = walk(2 * j + odd, [(qf[same, :], kf, vf), (qs[...], ks, vs)])
+    of[same, :] = finish(first)
+    os[...] = finish(second)
+    (third,) = walk(2 * j + 1 - odd, [(qf[other, :], kf, vf)])
+    of[other, :] = finish(third)
+
+
+def body_spread(n, queries, keys, values, frame_of_block, pair_mask, w_out):
+    tok, width = queries.shape
+    count_blocks = pair_mask.shape[1]
+    tokens = n * tok
+    per = tok // BLK
+    w_all = lax.all_gather(w_out, "seq", axis=1, tiled=True)
+    meta = jnp.concatenate([frame_of_block[:, None], pair_mask], axis=1)
+    meta = jnp.pad(meta, ((0, 8 - per), (0, HD - 1 - count_blocks)))
+    anyspace = pl.BlockSpec(memory_space=pl.ANY)
+    big = jax.ShapeDtypeStruct((tokens, HD), queries.dtype)
+    small = jax.ShapeDtypeStruct((tokens // 2, HD), queries.dtype)
+    qf, qs, kf, ks, vf, vs, metas = pl.pallas_call(
+        functools.partial(spread_kernel, n, tok),
+        out_shape=[big, small, big, big, big, big, jax.ShapeDtypeStruct((8 * n, HD), jnp.int32)],
+        in_specs=[anyspace] * 4,
+        out_specs=[anyspace] * 7,
+        scratch_shapes=[
+            pltpu.VMEM((5, tok, HD), queries.dtype),
+            pltpu.VMEM((tok // 2, HD), queries.dtype),
+            pltpu.VMEM((8, HD), jnp.int32),
+            pltpu.SemaphoreType.DMA((n - 1, 7)),
+            pltpu.SemaphoreType.DMA((n - 1, 7)),
+            pltpu.SemaphoreType.DMA((2, 7)),
+        ],
+        compiler_params=pltpu.CompilerParams(collective_id=0, has_side_effects=True),
+        cost_estimate=pl.CostEstimate(flops=0, bytes_accessed=300_000_000, transcendentals=0),
+        name="spread",
+    )(queries, keys, values, meta)
+
+    metas = metas.reshape(n, 8, HD)[:, :per].reshape(n * per, HD)
+    frame, links = metas[:, 0], metas[:, 1:1 + count_blocks]
+    allowed = (frame[None, :] <= frame[:, None]) & ((links == 1) | (frame[None, :] == frame[:, None]))
+    place = jnp.cumsum(allowed.astype(jnp.int32), axis=1)
+    count = place[:, -1]
+    ids = jnp.arange(count_blocks, dtype=jnp.int32)
+    hit = allowed[:, None, :] & (place[:, None, :] == ids[None, :, None] + 1)
+    order = jnp.sum(jnp.where(hit, ids[None, None, :], 0), axis=2)
+    odd = lax.rem(lax.axis_index("seq"), 2).reshape(1).astype(jnp.int32)
+
+    smem = pl.BlockSpec(memory_space=pltpu.SMEM)
+    whole = pl.BlockSpec((tokens, HD), lambda j: (0, 0))
+    two = pl.BlockSpec((2 * BLK, HD), lambda j: (j, 0))
+    one = pl.BlockSpec((BLK, HD), lambda j: (j, 0))
+    of, os = pl.pallas_call(
+        attend_kernel,
+        grid=(tokens // (2 * BLK),),
+        out_shape=[big, small],
+        in_specs=[smem, smem, smem, two, one, whole, whole, whole, whole],
+        out_specs=[two, one],
+        compiler_params=pltpu.CompilerParams(vmem_limit_bytes=48 * 1024 * 1024),
+        cost_estimate=pl.CostEstimate(flops=20_000_000_000, bytes_accessed=8_000_000, transcendentals=20_000_000),
+        name="attend",
+    )(odd, count, order, qf, qs, kf, ks, vf, vs)
+
+    attn = pl.pallas_call(
+        functools.partial(return_kernel, n, tok),
+        out_shape=jax.ShapeDtypeStruct((tok, width), queries.dtype),
+        in_specs=[anyspace] * 2,
+        out_specs=anyspace,
+        scratch_shapes=[
+            pltpu.VMEM((tok, HD), queries.dtype),
+            pltpu.VMEM((tok // 2, HD), queries.dtype),
+            pltpu.SemaphoreType.DMA((n - 1, 2)),
+            pltpu.SemaphoreType.DMA((n - 1, 2)),
+            pltpu.SemaphoreType.DMA((2, 2)),
+        ],
+        compiler_params=pltpu.CompilerParams(collective_id=1, has_side_effects=True),
+        cost_estimate=pl.CostEstimate(flops=0, bytes_accessed=100_000_000, transcendentals=0),
+        name="bring_back",
+    )(of, os)
+    terms = jnp.dot(attn, w_all, preferred_element_type=jnp.float32)
+    return lax.psum_scatter(terms.astype(jnp.bfloat16), "head", scatter_dimension=1, tiled=True)
+
+
+def body(n, queries, keys, values, frame_of_block, pair_mask, w_out):
+    heads_here = queries.shape[1] // HD
+    fits = n % 2 == 0 and 2 * heads_here == 3 * n and queries.shape[0] == 2 * BLK
+    if fits:
+        return body_spread(n, queries, keys, values, frame_of_block, pair_mask, w_out)
+    return body_gather(queries, keys, values, frame_of_block, pair_mask, w_out)
+
+
 def solution(mesh):
     placed = (
         P("seq", "head"),
@@ -87,5 +328,5 @@
         P("head", "seq"),
     )
     return jax.shard_map(
-        body, mesh=mesh, in_specs=placed, out_specs=P("seq", "head"), check_vma=False
+        functools.partial(body, mesh.shape["seq"]), mesh=mesh, in_specs=placed, out_specs=P("seq", "head"), check_vma=False
     )

time: 807 us -> 532 us (0.66)
  waiting for transfers between devices: 552 us -> 165 us
  Pallas kernels: 0 us -> 327 us
  matrix products: 163 us -> 15.9 us
  other arithmetic: 27.8 us -> 0.74 us
  blocking collectives: 24.2 us -> 0 us
  local copies, waits for them, and re-layouts: 25.3 us -> 8.22 us
    all_gather x3 -> x1, waiting for transfers between devices: 493 us -> 105 us  [body_spread(): w_all = lax.all_gather(w_out, 'seq', axis=1, tiled=True)]
    pallas_call x0 -> x3, Pallas kernels: none -> 327 us  [the longest x1 148 us: body_spread(): pl.pallas_call(functools.partial(spread_kernel, n, tok), out_shape=[big,...]
    dot_general x25 -> x1, matrix products: 163 us -> 15.9 us  [body_spread(): terms = jnp.dot(attn, w_all, preferred_element_type=jnp.float32)]
    reduce_sum x8 -> x1, other arithmetic: 25.1 us -> 0.42 us  [body_spread(): order = jnp.sum(jnp.where(hit, ids[None, None, :], 0), axis=2)]
    all_gather x1 -> x0, blocking collectives: 24.2 us -> none  [body(): k_frame = lax.all_gather(k_frame_local, 'seq', axis=0, tiled=True)]
    dynamic_slice x16 -> x0, local copies, waits for them, and re-layouts: 17.5 us -> none  [the longest x8 16.9 us: step(): lax.dynamic_slice_in_dim(v_rows, offset, key_span, 0)]
  transfers between devices with their start and end apart: 4 -> 2, of which waited for: 4 -> 2; matrix products, arithmetic and copies ran while one was open for 25% -> 0% of each run, Pallas kernels for 0% -> 62%
where the time goes in v1:
time: 532 us; the launch traced here: 530 us
  Pallas kernels  327 us (61%)
  waiting for transfers between devices  165 us (31%)
  matrix products  15.9 us (3%)
  between operations  13.5 us (3%)
  local copies, waits for them, and re-layouts  8.22 us (2%)
    pallas_call x1, Pallas kernels, body_spread(): pl.pallas_call(functools.partial(spread_kernel, n, tok), out_shape=[big,...  148 us
    pallas_call x1, Pallas kernels, body_spread(): pl.pallas_call(functools.partial(return_kernel, n, tok), out_shape=jax.Sh...  136 us
    all_gather x1, waiting for transfers between devices, body_spread(): w_all = lax.all_gather(w_out, 'seq', axis=1, tiled=True)  105 us
    reduce_scatter x1, waiting for transfers between devices, body_spread(): lax.psum_scatter(terms.astype(jnp.bfloat16), 'head', scatter_dimension=1,...  59.5 us
    pallas_call x1, Pallas kernels, body_spread(): pl.pallas_call(attend_kernel, grid=(tokens // (2 * BLK),), out_shape=[big...  43.5 us
    dot_general x1, matrix products, body_spread(): terms = jnp.dot(attn, w_all, preferred_element_type=jnp.float32)  15.9 us
  transfers between devices with their start and end apart: 2, of which 2 were waited for; matrix products, arithmetic and copies ran while one was open for 0% of the time, Pallas kernels for 62%

profile of v1, /device:TPU:1, one launch (start us, length us, event | category | flops | bytes accessed | tf_op | source)
XLA Modules:
  0.0 530.5 jit_solution(14379846726530737275)
XLA Ops:
  6.5 0.7 all-gather.2.cloned.1.call-update
  7.3 0.0 reduce-scatter.2.cloned.1.call-start
  7.3 0.1 copy.13
  7.4 0.1 pad_add_fusion
  7.5 0.6 pad.4.meta
  8.1 147.7 %spread.1 = (bf16[4096,128]{1,0:T(8,128)(2,1)}, bf16[2048,128]{1,0:T(8,128)(2,1)}, bf16[4096,128]{1,0:T(8,128)(2,1)}, bf16[4096,128]{1,0:T(8,128)(2,1)}, bf16[40...) custom-call(bf16[512,1536]{1,0:T(8,128)(2,1)} %q.1, bf16[512,1536]{1,0:T(8,128)(2,1)} %k.1, ...), custom_call_target="tpu_custom_call" | custom-call | bytes 300000000 | tf_op jit(solution)/shard_map/spread/pallas_call | solution.py:250
  155.8 0.8 slice.16
  156.5 0.1 slice_reduce_fusion.1
  156.7 0.1 fusion.2
  156.7 0.2 reduce_window_sum.11
  156.9 0.2 slice_reduce_fusion.count_ref
  157.1 0.4 select_reduce_fusion.list_ref
  157.5 1.2 copy-done.2
  158.8 1.2 copy-done.3
  160.0 1.2 copy-done.4
  161.2 1.0 copy-done.5
  162.2 43.5 %attend.1 = (bf16[4096,128]{1,0:T(8,128)(2,1)S(1)}, bf16[2048,128]{1,0:T(8,128)(2,1)S(1)}) custom-call(s32[1]{0:T(128)} %bitcast.odd_ref, s32[16]{0:T(128)S(1)} %slice_reduce_fusion.count_ref, s32[16,16]{1,0:T(8,128)S(1)} %select_reduce_fusion.list_ref, bf16[4096,128]{1,0:T(8,128)(2,1)S(1)} %copy-done.2, bf16[2048,128]{1,0:T(8,128)(2,1)S(1)} %copy-done.5, ...), custom_call_target="tpu_custom_call" | custom-call | flops 20000000000 | bytes 8000000 | tf_op jit(solution)/shard_map/attend/pallas_call | solution.py:282
  205.8 1.0 copy-done
  206.7 0.8 copy-done.1
  207.5 135.9 %bring_back.1 = bf16[512,1536]{1,0:T(8,128)(2,1)} custom-call(bf16[4096,128]{1,0:T(8,128)(2,1)} %copy-done, bf16[2048,128]{1,0:T(8,128)(2,1)} %copy-done.1), custom_call_target="tpu_custom_call" | custom-call | bytes 100000000 | tf_op jit(solution)/shard_map/bring_back/pallas_call | solution.py:293
  343.4 104.8 %all-gather.2.cloned.1.call-done = bf16[1536,6144]{1,0:T(8,128)(2,1)} async-done(((bf16[1536,768]{1,0:T(8,128)(2,1)}), bf16[1536,6144]{1,0:T(8,128)(2,1)}) %all-gather.2.cloned.1.call-update) | async-done | bytes 18874384 | tf_op jit(solution)/shard_map/all_gather | solution.py:244
  448.2 15.9 %convolution_convert_fusion = bf16[512,6144]{1,0:T(8,128)(2,1)} fusion(bf16[512,1536]{1,0:T(8,128)(2,1)} %bring_back.1, bf16[1536,6144]{1,0:T(8,128)(2,1)} %all-gather.2.cloned.1.call-done), kind=kOutput, calls=%fused_computation | convolution fusion | flops 9666822144 | bytes 26738688 | tf_op jit(solution)/shard_map/dot_general | solution.py:309
  464.1 0.0 reduce-scatter.2.cloned.1.call-update
  464.2 59.5 %reduce-scatter.2.cloned.1.call-done = bf16[512,1536]{1,0:T(8,128)(2,1)} async-done(((bf16[512,6144]{1,0:T(8,128)(2,1)}), bf16[512,1536]{1,0:T(8,128)(2,1)}) %reduce-scatter.2.cloned.1.call-update) | async-done | bytes 1572880 | tf_op jit(solution)/shard_map/reduce_scatter | solution.py:310
  (12 shorter events, 0.0 us)
Async XLA Ops:
  6.5 0.8 copy-start.7
  6.5 0.9 copy-start.6
  6.5 441.7 %all-gather.2.cloned.1.call-start = ((), (), s32[]{:S(2)}) async-start(), calls=%async_computation.1 | async-start | bytes 21233664 | tf_op jit(solution)/shard_map/all_gather | solution.py:244
  7.3 516.4 %reduce-scatter.2.cloned.1.call-start = ((), (), s32[]{:S(2)}) async-start(), calls=%async_computation.2 | async-start | bytes 7864320 | tf_op jit(solution)/shard_map/reduce_scatter | solution.py:310
  157.5 1.2 copy-start.2
  158.8 1.2 copy-start.3
  160.0 1.2 copy-start.4
  161.2 1.0 copy-start.5
  205.7 1.0 copy-start
  206.7 0.8 copy-start.1
Sparse Core Ops, SparseCore 0:
  8.9 439.3 all-gather.1
  464.3 59.3 reduce-scatter.1

commit v2 on v1

--- a/solution.py
+++ b/solution.py
@@ -146,43 +146,9 @@
         c.wait()
 
 
-def return_kernel(n, tok, of, os, attn, hold, hold_half, send, recv, here):
-    me = lax.axis_index("seq")
-    half = tok // 2
-    pair, odd = me // 2, lax.rem(me, 2)
-    own, shared = cols(3 * pair + 2 * odd), cols(3 * pair + 1)
-
-    def pieces(to):
-        return [
-            (of.at[rows(to * tok, tok)], attn.at[:, own]),
-            (os.at[rows(to * half, half)], attn.at[rows(odd * half, half), shared]),
-        ]
-
-    greet(n, me)
-    copies = []
-    for step in range(1, n):
-        to = lax.rem(me + step, n)
-        for i, (src, dst) in enumerate(pieces(to)):
-            copy = pltpu.make_async_remote_copy(
-                src_ref=src, dst_ref=dst, send_sem=send.at[step - 1, i], recv_sem=recv.at[step - 1, i],
-                device_id={"seq": to}, device_id_type=pl.DeviceIdType.MESH,
-            )
-            copy.start()
-            copies.append(copy)
-    for i, ((src, dst), via) in enumerate(zip(pieces(me), (hold, hold_half))):
-        c = pltpu.make_async_copy(src, via, here.at[0, i])
-        c.start()
-        c.wait()
-        d = pltpu.make_async_copy(via, dst, here.at[1, i])
-        d.start()
-        d.wait()
-    for c in copies:
-        c.wait()
-
-
-def attend_kernel(odd_ref, count_ref, list_ref, qf, qs, kf, ks, vf, vs, of, os):
+def attend_kernel(first_pair, odd_ref, count_ref, list_ref, qf, qs, kf, ks, vf, vs, of, os):
     odd = odd_ref[0]
-    j = pl.program_id(0)
+    j = pl.program_id(0) + first_pair
     factor = math.log2(math.e) / math.sqrt(HD)
 
     def scores(q, k):
@@ -236,12 +202,19 @@
     of[other, :] = finish(third)
 
 
+def project_kernel(pairs, whole_heads, shared_heads, w, out):
+    parts = []
+    for p in range(pairs):
+        parts += [whole_heads[p, 0], shared_heads[p, 0], whole_heads[p, 1]]
+    attn = jnp.concatenate(parts, axis=1)
+    out[...] = jnp.dot(attn, w[...], preferred_element_type=jnp.float32).astype(out.dtype)
+
+
 def body_spread(n, queries, keys, values, frame_of_block, pair_mask, w_out):
     tok, width = queries.shape
     count_blocks = pair_mask.shape[1]
     tokens = n * tok
     per = tok // BLK
-    w_all = lax.all_gather(w_out, "seq", axis=1, tiled=True)
     meta = jnp.concatenate([frame_of_block[:, None], pair_mask], axis=1)
     meta = jnp.pad(meta, ((0, 8 - per), (0, HD - 1 - count_blocks)))
     anyspace = pl.BlockSpec(memory_space=pl.ANY)
@@ -277,42 +250,77 @@
 
     smem = pl.BlockSpec(memory_space=pltpu.SMEM)
     whole = pl.BlockSpec((tokens, HD), lambda j: (0, 0))
-    two = pl.BlockSpec((2 * BLK, HD), lambda j: (j, 0))
-    one = pl.BlockSpec((BLK, HD), lambda j: (j, 0))
-    of, os = pl.pallas_call(
-        attend_kernel,
-        grid=(tokens // (2 * BLK),),
-        out_shape=[big, small],
-        in_specs=[smem, smem, smem, two, one, whole, whole, whole, whole],
-        out_specs=[two, one],
-        compiler_params=pltpu.CompilerParams(vmem_limit_bytes=48 * 1024 * 1024),
-        cost_estimate=pl.CostEstimate(flops=20_000_000_000, bytes_accessed=8_000_000, transcendentals=20_000_000),
-        name="attend",
-    )(odd, count, order, qf, qs, kf, ks, vf, vs)
-
-    attn = pl.pallas_call(
-        functools.partial(return_kernel, n, tok),
-        out_shape=jax.ShapeDtypeStruct((tok, width), queries.dtype),
-        in_specs=[anyspace] * 2,
-        out_specs=anyspace,
-        scratch_shapes=[
-            pltpu.VMEM((tok, HD), queries.dtype),
-            pltpu.VMEM((tok // 2, HD), queries.dtype),
-            pltpu.SemaphoreType.DMA((n - 1, 2)),
-            pltpu.SemaphoreType.DMA((n - 1, 2)),
-            pltpu.SemaphoreType.DMA((2, 2)),
-        ],
-        compiler_params=pltpu.CompilerParams(collective_id=1, has_side_effects=True),
-        cost_estimate=pl.CostEstimate(flops=0, bytes_accessed=100_000_000, transcendentals=0),
-        name="bring_back",
-    )(of, os)
-    terms = jnp.dot(attn, w_all, preferred_element_type=jnp.float32)
-    return lax.psum_scatter(terms.astype(jnp.bfloat16), "head", scatter_dimension=1, tiled=True)
-
-
-def body(n, queries, keys, values, frame_of_block, pair_mask, w_out):
+    pairs = n // 2
+    span = tokens // 2
+    sums = []
+    for part in range(2):
+        first = part * pairs
+        of, os = pl.pallas_call(
+            functools.partial(attend_kernel, first),
+            grid=(pairs,),
+            out_shape=[
+                jax.ShapeDtypeStruct((span, HD), queries.dtype),
+                jax.ShapeDtypeStruct((span // 2, HD), queries.dtype),
+            ],
+            in_specs=[
+                smem,
+                smem,
+                smem,
+                pl.BlockSpec((2 * BLK, HD), lambda j, first=first: (j + first, 0)),
+                pl.BlockSpec((BLK, HD), lambda j, first=first: (j + first, 0)),
+                whole,
+                whole,
+                whole,
+                whole,
+            ],
+            out_specs=[pl.BlockSpec((2 * BLK, HD), lambda j: (j, 0)), pl.BlockSpec((BLK, HD), lambda j: (j, 0))],
+            compiler_params=pltpu.CompilerParams(vmem_limit_bytes=40 * 1024 * 1024),
+            cost_estimate=pl.CostEstimate(
+                flops=(1 + 2 * part) * 7_000_000_000, bytes_accessed=8_000_000, transcendentals=8_000_000
+            ),
+            name=f"attend_{part}",
+        )(odd, count, order, qf, qs, kf, ks, vf, vs)
+        count, of = lax.optimization_barrier((count, of))
+        got = lax.all_gather(jnp.concatenate([of, os], axis=0), "seq", axis=0, tiled=True)
+        got = got.reshape(pairs, 2, span + span // 2, HD)
+        terms = pl.pallas_call(
+            functools.partial(project_kernel, pairs),
+            grid=(span // BLK,),
+            out_shape=jax.ShapeDtypeStruct((span, w_out.shape[1]), queries.dtype),
+            in_specs=[
+                pl.BlockSpec((pairs, 2, BLK, HD), lambda b: (0, 0, b, 0)),
+                pl.BlockSpec((pairs, 1, BLK, HD), lambda b: (0, lax.rem(b, 2), span // BLK + b // 2, 0)),
+                pl.BlockSpec(w_out.shape, lambda b: (0, 0)),
+            ],
+            out_specs=pl.BlockSpec((BLK, w_out.shape[1]), lambda b: (b, 0)),
+            compiler_params=pltpu.CompilerParams(vmem_limit_bytes=24 * 1024 * 1024),
+            cost_estimate=pl.CostEstimate(
+                flops=2 * span * width * w_out.shape[1], bytes_accessed=12_000_000, transcendentals=0
+            ),
+            name=f"project_{part}",
+        )(got, got, w_out)
+        sums.append(lax.psum_scatter(terms, "head", scatter_dimension=0, tiled=True))
+
+    heads = n // 2
+    at = lax.axis_index("seq")
+    came = []
+    for turn in range(2):
+        perm = []
+        for s in range(n):
+            for h in range(heads):
+                part = (s + turn) % 2
+                perm.append((s * heads + h, (part * heads + h) * heads + s // 2))
+        block = jnp.where(lax.rem(at + turn, 2) == 0, sums[0], sums[1])
+        came.append(lax.ppermute(block, ("seq", "head"), perm))
+    swap = at // heads == 1
+    left = jnp.where(swap, came[1], came[0])
+    right = jnp.where(swap, came[0], came[1])
+    return jnp.concatenate([left, right], axis=1)
+
+
+def body(n, heads_axis, queries, keys, values, frame_of_block, pair_mask, w_out):
     heads_here = queries.shape[1] // HD
-    fits = n % 2 == 0 and 2 * heads_here == 3 * n and queries.shape[0] == 2 * BLK
+    fits = n % 2 == 0 and 2 * heads_here == 3 * n and queries.shape[0] == 2 * BLK and 2 * heads_axis == n
     if fits:
         return body_spread(n, queries, keys, values, frame_of_block, pair_mask, w_out)
     return body_gather(queries, keys, values, frame_of_block, pair_mask, w_out)
@@ -328,5 +336,5 @@
         P("head", "seq"),
     )
     return jax.shard_map(
-        functools.partial(body, mesh.shape["seq"]), mesh=mesh, in_specs=placed, out_specs=P("seq", "head"), check_vma=False
+        functools.partial(body, mesh.shape["seq"], mesh.shape["head"]), mesh=mesh, in_specs=placed, out_specs=P("seq", "head"), check_vma=False
     )

time: 532 us -> 537 us (level)
  waiting for transfers between devices: 165 us -> 338 us
  Pallas kernels: 327 us -> 157 us
  matrix products: 15.9 us -> 0 us
  local copies, waits for them, and re-layouts: 8.22 us -> 15.1 us
  starting transfers between devices: 0.04 us -> 5.84 us
  other arithmetic: 0.74 us -> 6.19 us
    pallas_call x2 -> x4, Pallas kernels: 179 us -> 58.3 us  [the longest x2 43 us: body_spread(): pl.pallas_call(functools.partial(attend_kernel, first), grid=(pairs,), ou...]
    all_gather x1 -> x2, waiting for transfers between devices: 105 us -> 218 us  [body_spread(): lax.all_gather(jnp.concatenate([of, os], axis=0), 'seq', axis=0, tiled=True)]
    ppermute x0 -> x2, waiting for transfers between devices: none -> 51.1 us  [body_spread(): came.append(lax.ppermute(block, ('seq', 'head'), perm))]
    pallas_call x1, Pallas kernels: 148 us -> 99.1 us  [body_spread(): pl.pallas_call(functools.partial(spread_kernel, n, tok), out_shape=[big,...]
    dot_general x1 -> x0, matrix products: 15.9 us -> none  [body_spread(): terms = jnp.dot(attn, w_all, preferred_element_type=jnp.float32)]
    reduce_scatter x1 -> x2, waiting for transfers between devices: 59.5 us -> 69.7 us  [body_spread(): lax.psum_scatter(terms, 'head', scatter_dimension=0, tiled=True)]
    unnamed x16 -> x18, local copies, waits for them, and re-layouts: 6.47 us -> 12.7 us
    ppermute x0 -> x2, starting transfers between devices: none -> 5.71 us  [body_spread(): came.append(lax.ppermute(block, ('seq', 'head'), perm))]
  transfers between devices with their start and end apart: 2 -> 6, of which waited for: 2 -> 6; matrix products, arithmetic and copies ran while one was open for 0% -> 0% of each run, Pallas kernels for 62% -> 3%
where the time goes in v2:
time: 537 us; the launch traced here: 536 us
  waiting for transfers between devices  338 us (63%)
  Pallas kernels  157 us (29%)
  local copies, waits for them, and re-layouts  15.1 us (3%)
  between operations  13.2 us (2%)
  other arithmetic  6.19 us (1%)
  starting transfers between devices  5.84 us (1%)
    all_gather x2, waiting for transfers between devices, body_spread(): lax.all_gather(jnp.concatenate([of, os], axis=0), 'seq', axis=0, tiled=True)  218 us
    pallas_call x1, Pallas kernels, body_spread(): pl.pallas_call(functools.partial(spread_kernel, n, tok), out_shape=[big,...  99.1 us
    reduce_scatter x2, waiting for transfers between devices, body_spread(): lax.psum_scatter(terms, 'head', scatter_dimension=0, tiled=True)  69.7 us
    ppermute x2, waiting for transfers between devices, body_spread(): came.append(lax.ppermute(block, ('seq', 'head'), perm))  51.1 us
    pallas_call x2, Pallas kernels, body_spread(): pl.pallas_call(functools.partial(attend_kernel, first), grid=(pairs,), ou...  43 us
    pallas_call x2, Pallas kernels, body_spread(): pl.pallas_call(functools.partial(project_kernel, pairs), grid=(span // BL...  15.3 us
    unnamed x18, local copies, waits for them, and re-layouts  12.7 us
  transfers between devices with their start and end apart: 6, of which 6 were waited for; matrix products, arithmetic and copies ran while one was open for 0% of the time, Pallas kernels for 3%

profile of v2, /device:TPU:1, one launch (start us, length us, event | category | flops | bytes accessed | tf_op | source)
XLA Modules:
  0.0 536.1 jit_solution(7311989065370320950)
XLA Ops:
  8.6 99.1 %spread.1 = (bf16[4096,128]{1,0:T(8,128)(2,1)}, bf16[2048,128]{1,0:T(8,128)(2,1)}, bf16[4096,128]{1,0:T(8,128)(2,1)}, bf16[4096,128]{1,0:T(8,128)(2,1)}, bf16[40...) custom-call(bf16[512,1536]{1,0:T(8,128)(2,1)} %q.1, bf16[512,1536]{1,0:T(8,128)(2,1)} %k.1, ...), custom_call_target="tpu_custom_call" | custom-call | bytes 300000000 | tf_op jit(solution)/shard_map/spread/pallas_call | solution.py:223
  109.4 1.2 copy-done.3
  110.7 1.2 copy-done.4
  111.9 1.2 copy-done.5
  113.1 1.2 copy-done.6
  114.3 1.2 copy-done.7
  115.6 1.0 copy-done.8
  116.6 12.6 %attend_0.1 = (bf16[2048,128]{1,0:T(8,128)(2,1)S(1)}, bf16[1024,128]{1,0:T(8,128)(2,1)S(1)}) custom-call(s32[1]{0:T(128)} %bitcast.3.odd_ref, s32[16]{0:T(128)S(1)} %slice_reduce_fusion.count_ref, s32[16,16]{1,0:T(8,128)S(1)} %select_reduce_fusion.list_ref, bf16[4096,128]{1,0:T(8,128)(2,1)S(1)} %copy-done.3, bf16[2048,128]{1,0:T(8,128)(2,1)S(1)} %copy-done.8, ...), custom_call_target="tpu_custom_call" | custom-call | flops 7000000000 | bytes 8000000 | tf_op jit(solution)/shard_map/attend_0/pallas_call | solution.py:258
  129.2 30.4 %attend_1.1 = (bf16[2048,128]{1,0:T(8,128)(2,1)S(1)}, bf16[1024,128]{1,0:T(8,128)(2,1)S(1)}) custom-call(s32[1]{0:T(128)} %bitcast.3.odd_ref, s32[16]{0:T(128)S(1)} %slice_reduce_fusion.count_ref, s32[16,16]{1,0:T(8,128)S(1)} %select_reduce_fusion.list_ref, bf16[4096,128]{1,0:T(8,128)(2,1)S(1)} %copy-done.3, bf16[2048,128]{1,0:T(8,128)(2,1)S(1)} %copy-done.8, ...), custom_call_target="tpu_custom_call" | custom-call | flops 20999999488 | bytes 8000000 | tf_op jit(solution)/shard_map/attend_1/pallas_call | solution.py:258
  159.7 1.0 pad_maximum_fusion.2
  161.7 129.0 %all-gather.5.cloned.1.call-done = bf16[24576,128]{1,0:T(8,128)(2,1)} async-done(((bf16[3072,128]{1,0:T(8,128)(2,1)}), bf16[24576,128]{1,0:T(8,128)(2,1)}) %all-gather.5.cloned.1.call-update) | async-done | bytes 6291472 | tf_op jit(solution)/shard_map/all_gather | solution.py:284
  290.7 2.8 copy-done.1
  293.5 7.6 %project_1.1 = bf16[2048,768]{1,0:T(8,128)(2,1)} custom-call(bf16[4,2,3072,128]{3,2,1,0:T(8,128)(2,1)S(1)} %bitcast.8, bf16[4,2,3072,128]{3,2,1,0:T(8,128)(2,1)S(1)} %bitcast.9, bf16[1536,768]{1,0:T(8,128)(2,1)S(1)} %copy-done.2), custom_call_target="tpu_custom_call" | custom-call | flops 4831838208 | bytes 12000000 | tf_op jit(solution)/shard_map/project_1/pallas_call | solution.py:286
  301.2 88.6 %all-gather.3.cloned.1.call-done = bf16[24576,128]{1,0:T(8,128)(2,1)} async-done(((bf16[3072,128]{1,0:T(8,128)(2,1)}), bf16[24576,128]{1,0:T(8,128)(2,1)}) %all-gather.3.cloned.1.call-update) | async-done | bytes 6291472 | tf_op jit(solution)/shard_map/all_gather | solution.py:284
  389.8 2.8 copy-done
  392.6 7.6 %project_0.1 = bf16[2048,768]{1,0:T(8,128)(2,1)} custom-call(bf16[4,2,3072,128]{3,2,1,0:T(8,128)(2,1)S(1)} %bitcast.6, bf16[4,2,3072,128]{3,2,1,0:T(8,128)(2,1)S(1)} %bitcast.7, bf16[1536,768]{1,0:T(8,128)(2,1)S(1)} %copy-done.2), custom_call_target="tpu_custom_call" | custom-call | flops 4831838208 | bytes 12000000 | tf_op jit(solution)/shard_map/project_0/pallas_call | solution.py:286
  400.2 29.4 %reduce-scatter.5.cloned.1.call-done = bf16[512,768]{1,0:T(8,128)(2,1)} async-done(((bf16[2048,768]{1,0:T(8,128)(2,1)}), bf16[512,768]{1,0:T(8,128)(2,1)}) %reduce-scatter.5.cloned.1.call-update) | async-done | bytes 786448 | tf_op jit(solution)/shard_map/reduce_scatter | solution.py:302
  429.6 40.3 %reduce-scatter.3.cloned.1.call-done = bf16[512,768]{1,0:T(8,128)(2,1)} async-done(((bf16[2048,768]{1,0:T(8,128)(2,1)}), bf16[512,768]{1,0:T(8,128)(2,1)}) %reduce-scatter.3.cloned.1.call-update) | async-done | bytes 786448 | tf_op jit(solution)/shard_map/reduce_scatter | solution.py:302
  469.9 1.5 broadcast_select_fusion.1
  471.4 3.8 collective-permute-start
  475.2 1.9 collective-permute-start.1
  477.2 48.2 %collective-permute-done = bf16[512,768]{1,0:T(8,128)(2,1)S(1)} collective-permute-done((bf16[512,768]{1,0:T(8,128)(2,1)S(1)}, bf16[512,768]{1,0:T(8,128)(2,1)S(1)}, u32[]{:S(2)}, u32[]{:S(2)}) %collective-permute-start) | collective-permute-done | bytes 786464 | tf_op jit(solution)/shard_map/ppermute | solution.py:314
  525.3 2.9 collective-permute-done.1
  528.3 1.3 pad_maximum_fusion
  (30 shorter events, 5.1 us)
Async XLA Ops:
  6.5 284.2 %all-gather.5.cloned.1.call-start = ((), (), s32[]{:S(2)}) async-start(), calls=%async_computation.4 | async-start | bytes 7077888 | tf_op jit(solution)/shard_map/all_gather | solution.py:284
  109.4 1.2 copy-start.3
  110.7 1.2 copy-start.4
  111.9 1.2 copy-start.5
  113.1 1.2 copy-start.6
  114.3 1.2 copy-start.7
  115.6 1.0 copy-start.8
  160.7 130.0 %copy-start.2 = (bf16[1536,768]{1,0:T(8,128)(2,1)S(1)}, bf16[1536,768]{1,0:T(8,128)(2,1)}, u32[]{:S(2)}) copy-start(bf16[1536,768]{1,0:T(8,128)(2,1)} %w.3) | copy-start | bytes 7077892
  160.7 229.1 %all-gather.3.cloned.1.call-start = ((), (), s32[]{:S(2)}) async-start(), calls=%async_computation.2 | async-start | bytes 7077888 | tf_op jit(solution)/shard_map/all_gather | solution.py:284
  161.7 267.9 %reduce-scatter.5.cloned.1.call-start = ((), (), s32[]{:S(2)}) async-start(), calls=%async_computation.5 | async-start | bytes 3932160 | tf_op jit(solution)/shard_map/reduce_scatter | solution.py:302
  290.7 2.8 copy-start.1
  301.2 168.8 %reduce-scatter.3.cloned.1.call-start = ((), (), s32[]{:S(2)}) async-start(), calls=%async_computation.3 | async-start | bytes 3932160 | tf_op jit(solution)/shard_map/reduce_scatter | solution.py:302
  389.8 2.8 copy-start
  471.4 53.9 %collective-permute-start = (bf16[512,768]{1,0:T(8,128)(2,1)S(1)}, bf16[512,768]{1,0:T(8,128)(2,1)S(1)}, u32[]{:S(2)}, u32[]{:S(2)}) collective-permute-start(bf16[512,768]{1,0:T(8,128)(2,1)S(1)} %get-tuple-element.37), channel_id=1, source_target_pairs={{0,16},{1,20},{2,24},{3,28},{4,0},{5,4},{6,8},{7,12},{8,17},{9,21}... | collective-permute-start | bytes 2359304 | tf_op jit(solution)/shard_map/ppermute | solution.py:314
  475.2 53.0 %collective-permute-start.1 = (bf16[512,768]{1,0:T(8,128)(2,1)S(1)}, bf16[512,768]{1,0:T(8,128)(2,1)S(1)}, u32[]{:S(2)}, u32[]{:S(2)}) collective-permute-start(bf16[512,768]{1,0:T(8,128)(2,1)S(1)} %get-tuple-element.38), channel_id=1, source_target_pairs={{0,0},{1,4},{2,8},{3,12},{4,16},{5,20},{6,24},{7,28},{8,1},{9,5},{... | collective-permute-start | bytes 2359304 | tf_op jit(solution)/shard_map/ppermute | solution.py:314
Sparse Core Ops, SparseCore 0:
  160.8 129.8 all-gather.4
  292.9 96.8 all-gather.2
  392.3 37.2 reduce-scatter.4
  432.0 37.8 reduce-scatter.2
